TPU v7x, 32 devices: a 4x4x1 block of a 4x4x8 slice. The times are simulated.
32 devices in a mesh: dp: 1 (over z), ep: 32 (over y, x, core).
Axes of the slice: x: 4, y: 4, z: 1, core: 2. Of those that a mesh axis runs over, the one named last changes fastest.
The devices are a block of a 4x4x8 slice.
Arguments:
- tokens: bfloat16 [24576, 1024], P(('dp', 'ep'))
- expert_ids: int32 [24576, 8], P(('dp', 'ep'))
- gate_wts: float32 [24576, 8], P(('dp', 'ep'))
- slot_ids: int32 [24576, 8], P(('dp', 'ep'))
- w_gate: bfloat16 [32, 1024, 512], P('ep')
- w_up: bfloat16 [32, 1024, 512], P('ep')
- w_down: bfloat16 [32, 512, 1024], P('ep')
Outputs:
- output: bfloat16 [24576, 1024], P(('dp', 'ep'))
All inputs are finite; a program needn't handle non-finite values.
Results may differ from a plain program's by a relative error of at most 0.001.
Values are sent between devices in bfloat16 or wider.
A program may use at most 768 MiB of HBM per device.

v0:
```python
import functools
import jax
import jax.numpy as jnp
from jax import lax
from jax.sharding import PartitionSpec as P

CAP_NUM = 3
CAP_DEN = 2


def local_share(token_block, src_shard, my_rank, w_gate, w_up, w_down, shard_cap):
    token_blk, ids_blk, gates_blk, slots_blk = token_block
    num_local = w_gate.shape[0]
    tok_dev = token_blk.shape[0]
    local_id = ids_blk - my_rank * num_local
    keep_mask = (slots_blk >= 0) & (local_id >= 0) & (local_id < num_local)
    flat_slot = jnp.where(keep_mask, local_id * shard_cap + slots_blk - src_shard * shard_cap, num_local * shard_cap).reshape(-1)
    tok_index = jnp.broadcast_to(jnp.arange(tok_dev, dtype=jnp.int32)[:, None], ids_blk.shape).reshape(-1)
    slot_token = jnp.full((num_local * shard_cap,), tok_dev, jnp.int32).at[flat_slot].set(tok_index, mode='drop')
    slot_gate = jnp.zeros((num_local * shard_cap,), jnp.float32).at[flat_slot].set(gates_blk.reshape(-1), mode='drop')
    dispatched = jnp.take(token_blk, slot_token, axis=0, mode='fill', fill_value=0).reshape(num_local, shard_cap, -1)
    h_gate = jnp.einsum('ecd,edf->ecf', dispatched, w_gate, preferred_element_type=jnp.float32)
    h_up = jnp.einsum('ecd,edf->ecf', dispatched, w_up, preferred_element_type=jnp.float32)
    hidden = (jax.nn.silu(h_gate) * h_up).astype(jnp.bfloat16)
    expert_out = jnp.einsum('ecf,efd->ecd', hidden, w_down, preferred_element_type=jnp.float32)
    weighted = (expert_out * slot_gate.reshape(num_local, shard_cap, 1)).reshape(num_local * shard_cap, -1)
    return jnp.zeros((tok_dev, token_blk.shape[1]), jnp.float32).at[slot_token].add(weighted, mode='drop')


def solution(mesh):
    group_size = mesh.shape['ep']
    next_perm = [(dev_num, (dev_num + 1) % group_size) for dev_num in range(group_size)]
    row_spec = P(('dp', 'ep'), None)
    expert_spec = P('ep', None, None)

    def per_device(tokens, expert_ids, gate_wts, slot_ids, w_gate, w_up, w_down):
        my_rank = lax.axis_index('ep')
        tok_dev, top_k = expert_ids.shape
        shard_cap = CAP_NUM * tok_dev * top_k // (CAP_DEN * w_gate.shape[0] * group_size)
        expert_share = functools.partial(local_share, my_rank=my_rank, w_gate=w_gate, w_up=w_up, w_down=w_down, shard_cap=shard_cap)
        own_block = (tokens, expert_ids, gate_wts, slot_ids)
        home_part = expert_share(own_block, my_rank)
        visitor = lax.ppermute(own_block, 'ep', next_perm)
        accum = expert_share(visitor, (my_rank - 1) % group_size)

        def pass_on(hop_num, loop_state):
            visitor, accum = loop_state
            visitor, accum = lax.ppermute((visitor, accum), 'ep', next_perm)
            return visitor, accum + expert_share(visitor, (my_rank - hop_num) % group_size)

        visitor, accum = lax.fori_loop(2, group_size, pass_on, (visitor, accum))
        accum = lax.ppermute(accum, 'ep', next_perm)
        return (accum + home_part).astype(jnp.bfloat16)

    return jax.shard_map(per_device, mesh=mesh, in_specs=(row_spec, row_spec, row_spec, row_spec, expert_spec, expert_spec, expert_spec), out_specs=row_spec, check_vma=False)
```

profile of v0, /device:TPU:97, one launch (start us, length us, event | category | flops | bytes accessed | tf_op | source)
XLA Modules:
  0.0 3291.3 jit_solution(13445550603138043767)
XLA Ops:
  6.2 23.0 scatter_custom_fusion.3
  64.8 3157.6 %while.23 = (s32[]{:T(128)}, bf16[768,1024]{1,0:T(8,128)(2,1)}, s32[768,8]{0,1:T(8,128)S(1)}, f32[768,8]{1,0:T(8,128)S(1)}, s32[768,8]{0,1:T(8,128)S(1)}, /*inde...) while((s32[]{:T(128)}, bf16[768,1024]{1,0:T(8,128)(2,1)}, ...), condition=%wide.region_7.9_spmd, body=%wide.region_3.0_spmd.sunk | while | flops 908117504 | bytes 41303272 | solution.py:51
  70.0 30.7 collective-permute-done.1
  101.4 23.0 scatter_custom_fusion.26
  172.9 30.7 collective-permute-done.1
  204.4 23.0 scatter_custom_fusion.26
  275.9 30.7 collective-permute-done.1
  307.3 23.0 scatter_custom_fusion.26
  378.8 30.7 collective-permute-done.1
  410.3 23.0 scatter_custom_fusion.26
  481.8 30.7 collective-permute-done.1
  513.3 23.0 scatter_custom_fusion.26
  584.8 30.7 collective-permute-done.1
  616.2 23.0 scatter_custom_fusion.26
  687.7 30.7 collective-permute-done.1
  719.2 23.0 scatter_custom_fusion.26
  790.7 30.7 collective-permute-done.1
  822.2 23.0 scatter_custom_fusion.26
  893.7 30.9 collective-permute-done.1
  925.1 23.0 scatter_custom_fusion.26
  996.6 34.2 %collective-permute-done.1 = s32[768,8]{0,1:T(8,128)S(1)} collective-permute-done((s32[768,8]{0,1:T(8,128)S(1)}, s32[768,8]{0,1:T(8,128)S(1)}, u32[]{:S(2)}, u32[]{:S(2)}) %collective-permute-start.1) | collective-permute-done | bytes 24608 | tf_op jit(solution)/shard_map/while/body/eval_jaxpr/ppermute | solution.py:48
  1099.6 37.5 %collective-permute-done.1 = s32[768,8]{0,1:T(8,128)S(1)} collective-permute-done((s32[768,8]{0,1:T(8,128)S(1)}, s32[768,8]{0,1:T(8,128)S(1)}, u32[]{:S(2)}, u32[]{:S(2)}) %collective-permute-start.1) | collective-permute-done | bytes 24608 | tf_op jit(solution)/shard_map/while/body/eval_jaxpr/ppermute | solution.py:48
  1137.6 23.0 scatter_custom_fusion.26
  1203.4 40.0 %collective-permute-done.1 = s32[768,8]{0,1:T(8,128)S(1)} collective-permute-done((s32[768,8]{0,1:T(8,128)S(1)}, s32[768,8]{0,1:T(8,128)S(1)}, u32[]{:S(2)}, u32[]{:S(2)}) %collective-permute-start.1) | collective-permute-done | bytes 24608 | tf_op jit(solution)/shard_map/while/body/eval_jaxpr/ppermute | solution.py:48
  1243.9 23.0 scatter_custom_fusion.26
  1309.7 40.0 %collective-permute-done.1 = s32[768,8]{0,1:T(8,128)S(1)} collective-permute-done((s32[768,8]{0,1:T(8,128)S(1)}, s32[768,8]{0,1:T(8,128)S(1)}, u32[]{:S(2)}, u32[]{:S(2)}) %collective-permute-start.1) | collective-permute-done | bytes 24608 | tf_op jit(solution)/shard_map/while/body/eval_jaxpr/ppermute | solution.py:48
  1416.0 40.0 %collective-permute-done.1 = s32[768,8]{0,1:T(8,128)S(1)} collective-permute-done((s32[768,8]{0,1:T(8,128)S(1)}, s32[768,8]{0,1:T(8,128)S(1)}, u32[]{:S(2)}, u32[]{:S(2)}) %collective-permute-start.1) | collective-permute-done | bytes 24608 | tf_op jit(solution)/shard_map/while/body/eval_jaxpr/ppermute | solution.py:48
  1456.5 23.0 scatter_custom_fusion.26
  1522.3 40.0 %collective-permute-done.1 = s32[768,8]{0,1:T(8,128)S(1)} collective-permute-done((s32[768,8]{0,1:T(8,128)S(1)}, s32[768,8]{0,1:T(8,128)S(1)}, u32[]{:S(2)}, u32[]{:S(2)}) %collective-permute-start.1) | collective-permute-done | bytes 24608 | tf_op jit(solution)/shard_map/while/body/eval_jaxpr/ppermute | solution.py:48
  1562.8 23.0 scatter_custom_fusion.26
  1628.6 40.0 %collective-permute-done.1 = s32[768,8]{0,1:T(8,128)S(1)} collective-permute-done((s32[768,8]{0,1:T(8,128)S(1)}, s32[768,8]{0,1:T(8,128)S(1)}, u32[]{:S(2)}, u32[]{:S(2)}) %collective-permute-start.1) | collective-permute-done | bytes 24608 | tf_op jit(solution)/shard_map/while/body/eval_jaxpr/ppermute | solution.py:48
  1734.9 40.0 %collective-permute-done.1 = s32[768,8]{0,1:T(8,128)S(1)} collective-permute-done((s32[768,8]{0,1:T(8,128)S(1)}, s32[768,8]{0,1:T(8,128)S(1)}, u32[]{:S(2)}, u32[]{:S(2)}) %collective-permute-start.1) | collective-permute-done | bytes 24608 | tf_op jit(solution)/shard_map/while/body/eval_jaxpr/ppermute | solution.py:48
  1775.4 23.0 scatter_custom_fusion.26
  1841.2 40.0 %collective-permute-done.1 = s32[768,8]{0,1:T(8,128)S(1)} collective-permute-done((s32[768,8]{0,1:T(8,128)S(1)}, s32[768,8]{0,1:T(8,128)S(1)}, u32[]{:S(2)}, u32[]{:S(2)}) %collective-permute-start.1) | collective-permute-done | bytes 24608 | tf_op jit(solution)/shard_map/while/body/eval_jaxpr/ppermute | solution.py:48
  1947.5 40.0 %collective-permute-done.1 = s32[768,8]{0,1:T(8,128)S(1)} collective-permute-done((s32[768,8]{0,1:T(8,128)S(1)}, s32[768,8]{0,1:T(8,128)S(1)}, u32[]{:S(2)}, u32[]{:S(2)}) %collective-permute-start.1) | collective-permute-done | bytes 24608 | tf_op jit(solution)/shard_map/while/body/eval_jaxpr/ppermute | solution.py:48
  2053.8 40.0 %collective-permute-done.1 = s32[768,8]{0,1:T(8,128)S(1)} collective-permute-done((s32[768,8]{0,1:T(8,128)S(1)}, s32[768,8]{0,1:T(8,128)S(1)}, u32[]{:S(2)}, u32[]{:S(2)}) %collective-permute-start.1) | collective-permute-done | bytes 24608 | tf_op jit(solution)/shard_map/while/body/eval_jaxpr/ppermute | solution.py:48
  2160.0 40.0 %collective-permute-done.1 = s32[768,8]{0,1:T(8,128)S(1)} collective-permute-done((s32[768,8]{0,1:T(8,128)S(1)}, s32[768,8]{0,1:T(8,128)S(1)}, u32[]{:S(2)}, u32[]{:S(2)}) %collective-permute-start.1) | collective-permute-done | bytes 24608 | tf_op jit(solution)/shard_map/while/body/eval_jaxpr/ppermute | solution.py:48
  2266.3 40.0 %collective-permute-done.1 = s32[768,8]{0,1:T(8,128)S(1)} collective-permute-done((s32[768,8]{0,1:T(8,128)S(1)}, s32[768,8]{0,1:T(8,128)S(1)}, u32[]{:S(2)}, u32[]{:S(2)}) %collective-permute-start.1) | collective-permute-done | bytes 24608 | tf_op jit(solution)/shard_map/while/body/eval_jaxpr/ppermute | solution.py:48
  2372.6 40.0 %collective-permute-done.1 = s32[768,8]{0,1:T(8,128)S(1)} collective-permute-done((s32[768,8]{0,1:T(8,128)S(1)}, s32[768,8]{0,1:T(8,128)S(1)}, u32[]{:S(2)}, u32[]{:S(2)}) %collective-permute-start.1) | collective-permute-done | bytes 24608 | tf_op jit(solution)/shard_map/while/body/eval_jaxpr/ppermute | solution.py:48
  2478.9 40.0 %collective-permute-done.1 = s32[768,8]{0,1:T(8,128)S(1)} collective-permute-done((s32[768,8]{0,1:T(8,128)S(1)}, s32[768,8]{0,1:T(8,128)S(1)}, u32[]{:S(2)}, u32[]{:S(2)}) %collective-permute-start.1) | collective-permute-done | bytes 24608 | tf_op jit(solution)/shard_map/while/body/eval_jaxpr/ppermute | solution.py:48
  2585.2 40.0 %collective-permute-done.1 = s32[768,8]{0,1:T(8,128)S(1)} collective-permute-done((s32[768,8]{0,1:T(8,128)S(1)}, s32[768,8]{0,1:T(8,128)S(1)}, u32[]{:S(2)}, u32[]{:S(2)}) %collective-permute-start.1) | collective-permute-done | bytes 24608 | tf_op jit(solution)/shard_map/while/body/eval_jaxpr/ppermute | solution.py:48
  2691.5 40.0 %collective-permute-done.1 = s32[768,8]{0,1:T(8,128)S(1)} collective-permute-done((s32[768,8]{0,1:T(8,128)S(1)}, s32[768,8]{0,1:T(8,128)S(1)}, u32[]{:S(2)}, u32[]{:S(2)}) %collective-permute-start.1) | collective-permute-done | bytes 24608 | tf_op jit(solution)/shard_map/while/body/eval_jaxpr/ppermute | solution.py:48
  2797.8 40.0 %collective-permute-done.1 = s32[768,8]{0,1:T(8,128)S(1)} collective-permute-done((s32[768,8]{0,1:T(8,128)S(1)}, s32[768,8]{0,1:T(8,128)S(1)}, u32[]{:S(2)}, u32[]{:S(2)}) %collective-permute-start.1) | collective-permute-done | bytes 24608 | tf_op jit(solution)/shard_map/while/body/eval_jaxpr/ppermute | solution.py:48
  2904.1 40.0 %collective-permute-done.1 = s32[768,8]{0,1:T(8,128)S(1)} collective-permute-done((s32[768,8]{0,1:T(8,128)S(1)}, s32[768,8]{0,1:T(8,128)S(1)}, u32[]{:S(2)}, u32[]{:S(2)}) %collective-permute-start.1) | collective-permute-done | bytes 24608 | tf_op jit(solution)/shard_map/while/body/eval_jaxpr/ppermute | solution.py:48
  3010.4 40.0 %collective-permute-done.1 = s32[768,8]{0,1:T(8,128)S(1)} collective-permute-done((s32[768,8]{0,1:T(8,128)S(1)}, s32[768,8]{0,1:T(8,128)S(1)}, u32[]{:S(2)}, u32[]{:S(2)}) %collective-permute-start.1) | collective-permute-done | bytes 24608 | tf_op jit(solution)/shard_map/while/body/eval_jaxpr/ppermute | solution.py:48
  3116.7 40.0 %collective-permute-done.1 = s32[768,8]{0,1:T(8,128)S(1)} collective-permute-done((s32[768,8]{0,1:T(8,128)S(1)}, s32[768,8]{0,1:T(8,128)S(1)}, u32[]{:S(2)}, u32[]{:S(2)}) %collective-permute-start.1) | collective-permute-done | bytes 24608 | tf_op jit(solution)/shard_map/while/body/eval_jaxpr/ppermute | solution.py:48
  3227.1 23.1 scatter_custom_fusion.6
  3255.2 23.4 scatter_custom_fusion.7
  (929 shorter events, 1786.7 us)
Async XLA Ops:
  64.8 91.3 %collective-permute-start.4 = (f32[768,1024]{1,0:T(8,128)}, f32[768,1024]{1,0:T(8,128)}, u32[]{:S(2)}, u32[]{:S(2)}) collective-permute-start(f32[768,1024]{1,0:T(8,128)} %get-tuple-element.354), channel_id=1, source_target_pairs={{0,1},{1,2},{2,3},{3,4},{4,5},{5,6},{6,7},{7,8},{8,9},{9,10},{10,1... | collective-permute-start | bytes 9437192 | tf_op jit(solution)/shard_map/while/body/eval_jaxpr/ppermute | solution.py:48
  166.7 92.4 %collective-permute-start.4 = (f32[768,1024]{1,0:T(8,128)}, f32[768,1024]{1,0:T(8,128)}, u32[]{:S(2)}, u32[]{:S(2)}) collective-permute-start(f32[768,1024]{1,0:T(8,128)} %get-tuple-element.354), channel_id=1, source_target_pairs={{0,1},{1,2},{2,3},{3,4},{4,5},{5,6},{6,7},{7,8},{8,9},{9,10},{10,1... | collective-permute-start | bytes 9437192 | tf_op jit(solution)/shard_map/while/body/eval_jaxpr/ppermute | solution.py:48
  269.6 92.4 %collective-permute-start.4 = (f32[768,1024]{1,0:T(8,128)}, f32[768,1024]{1,0:T(8,128)}, u32[]{:S(2)}, u32[]{:S(2)}) collective-permute-start(f32[768,1024]{1,0:T(8,128)} %get-tuple-element.354), channel_id=1, source_target_pairs={{0,1},{1,2},{2,3},{3,4},{4,5},{5,6},{6,7},{7,8},{8,9},{9,10},{10,1... | collective-permute-start | bytes 9437192 | tf_op jit(solution)/shard_map/while/body/eval_jaxpr/ppermute | solution.py:48
  372.6 92.4 %collective-permute-start.4 = (f32[768,1024]{1,0:T(8,128)}, f32[768,1024]{1,0:T(8,128)}, u32[]{:S(2)}, u32[]{:S(2)}) collective-permute-start(f32[768,1024]{1,0:T(8,128)} %get-tuple-element.354), channel_id=1, source_target_pairs={{0,1},{1,2},{2,3},{3,4},{4,5},{5,6},{6,7},{7,8},{8,9},{9,10},{10,1... | collective-permute-start | bytes 9437192 | tf_op jit(solution)/shard_map/while/body/eval_jaxpr/ppermute | solution.py:48
  475.6 92.4 %collective-permute-start.4 = (f32[768,1024]{1,0:T(8,128)}, f32[768,1024]{1,0:T(8,128)}, u32[]{:S(2)}, u32[]{:S(2)}) collective-permute-start(f32[768,1024]{1,0:T(8,128)} %get-tuple-element.354), channel_id=1, source_target_pairs={{0,1},{1,2},{2,3},{3,4},{4,5},{5,6},{6,7},{7,8},{8,9},{9,10},{10,1... | collective-permute-start | bytes 9437192 | tf_op jit(solution)/shard_map/while/body/eval_jaxpr/ppermute | solution.py:48
  578.6 92.4 %collective-permute-start.4 = (f32[768,1024]{1,0:T(8,128)}, f32[768,1024]{1,0:T(8,128)}, u32[]{:S(2)}, u32[]{:S(2)}) collective-permute-start(f32[768,1024]{1,0:T(8,128)} %get-tuple-element.354), channel_id=1, source_target_pairs={{0,1},{1,2},{2,3},{3,4},{4,5},{5,6},{6,7},{7,8},{8,9},{9,10},{10,1... | collective-permute-start | bytes 9437192 | tf_op jit(solution)/shard_map/while/body/eval_jaxpr/ppermute | solution.py:48
  681.5 92.4 %collective-permute-start.4 = (f32[768,1024]{1,0:T(8,128)}, f32[768,1024]{1,0:T(8,128)}, u32[]{:S(2)}, u32[]{:S(2)}) collective-permute-start(f32[768,1024]{1,0:T(8,128)} %get-tuple-element.354), channel_id=1, source_target_pairs={{0,1},{1,2},{2,3},{3,4},{4,5},{5,6},{6,7},{7,8},{8,9},{9,10},{10,1... | collective-permute-start | bytes 9437192 | tf_op jit(solution)/shard_map/while/body/eval_jaxpr/ppermute | solution.py:48
  784.5 92.4 %collective-permute-start.4 = (f32[768,1024]{1,0:T(8,128)}, f32[768,1024]{1,0:T(8,128)}, u32[]{:S(2)}, u32[]{:S(2)}) collective-permute-start(f32[768,1024]{1,0:T(8,128)} %get-tuple-element.354), channel_id=1, source_target_pairs={{0,1},{1,2},{2,3},{3,4},{4,5},{5,6},{6,7},{7,8},{8,9},{9,10},{10,1... | collective-permute-start | bytes 9437192 | tf_op jit(solution)/shard_map/while/body/eval_jaxpr/ppermute | solution.py:48
  887.5 92.4 %collective-permute-start.4 = (f32[768,1024]{1,0:T(8,128)}, f32[768,1024]{1,0:T(8,128)}, u32[]{:S(2)}, u32[]{:S(2)}) collective-permute-start(f32[768,1024]{1,0:T(8,128)} %get-tuple-element.354), channel_id=1, source_target_pairs={{0,1},{1,2},{2,3},{3,4},{4,5},{5,6},{6,7},{7,8},{8,9},{9,10},{10,1... | collective-permute-start | bytes 9437192 | tf_op jit(solution)/shard_map/while/body/eval_jaxpr/ppermute | solution.py:48
  990.4 95.6 %collective-permute-start.4 = (f32[768,1024]{1,0:T(8,128)}, f32[768,1024]{1,0:T(8,128)}, u32[]{:S(2)}, u32[]{:S(2)}) collective-permute-start(f32[768,1024]{1,0:T(8,128)} %get-tuple-element.354), channel_id=1, source_target_pairs={{0,1},{1,2},{2,3},{3,4},{4,5},{5,6},{6,7},{7,8},{8,9},{9,10},{10,1... | collective-permute-start | bytes 9437192 | tf_op jit(solution)/shard_map/while/body/eval_jaxpr/ppermute | solution.py:48
  1096.6 95.7 %collective-permute-start.4 = (f32[768,1024]{1,0:T(8,128)}, f32[768,1024]{1,0:T(8,128)}, u32[]{:S(2)}, u32[]{:S(2)}) collective-permute-start(f32[768,1024]{1,0:T(8,128)} %get-tuple-element.354), channel_id=1, source_target_pairs={{0,1},{1,2},{2,3},{3,4},{4,5},{5,6},{6,7},{7,8},{8,9},{9,10},{10,1... | collective-permute-start | bytes 9437192 | tf_op jit(solution)/shard_map/while/body/eval_jaxpr/ppermute | solution.py:48
  1202.9 95.7 %collective-permute-start.4 = (f32[768,1024]{1,0:T(8,128)}, f32[768,1024]{1,0:T(8,128)}, u32[]{:S(2)}, u32[]{:S(2)}) collective-permute-start(f32[768,1024]{1,0:T(8,128)} %get-tuple-element.354), channel_id=1, source_target_pairs={{0,1},{1,2},{2,3},{3,4},{4,5},{5,6},{6,7},{7,8},{8,9},{9,10},{10,1... | collective-permute-start | bytes 9437192 | tf_op jit(solution)/shard_map/while/body/eval_jaxpr/ppermute | solution.py:48
  1202.9 87.2 %collective-permute-start = (bf16[768,1024]{1,0:T(8,128)(2,1)}, bf16[768,1024]{1,0:T(8,128)(2,1)S(1)}, u32[]{:S(2)}, u32[]{:S(2)}) collective-permute-start(bf16[768,1024]{1,0:T(8,128)(2,1)} %get-tuple-element.350), channel_id=1, source_target_pairs={{0,1},{1,2},{2,3},{3,4},{4,5},{5,6},{6,7},{7,8},{8,9},{9,10},{10,1... | collective-permute-start | bytes 4718600 | tf_op jit(solution)/shard_map/while/body/eval_jaxpr/ppermute | solution.py:48
  1309.2 95.7 %collective-permute-start.4 = (f32[768,1024]{1,0:T(8,128)}, f32[768,1024]{1,0:T(8,128)}, u32[]{:S(2)}, u32[]{:S(2)}) collective-permute-start(f32[768,1024]{1,0:T(8,128)} %get-tuple-element.354), channel_id=1, source_target_pairs={{0,1},{1,2},{2,3},{3,4},{4,5},{5,6},{6,7},{7,8},{8,9},{9,10},{10,1... | collective-permute-start | bytes 9437192 | tf_op jit(solution)/shard_map/while/body/eval_jaxpr/ppermute | solution.py:48
  1309.2 87.2 %collective-permute-start = (bf16[768,1024]{1,0:T(8,128)(2,1)}, bf16[768,1024]{1,0:T(8,128)(2,1)S(1)}, u32[]{:S(2)}, u32[]{:S(2)}) collective-permute-start(bf16[768,1024]{1,0:T(8,128)(2,1)} %get-tuple-element.350), channel_id=1, source_target_pairs={{0,1},{1,2},{2,3},{3,4},{4,5},{5,6},{6,7},{7,8},{8,9},{9,10},{10,1... | collective-permute-start | bytes 4718600 | tf_op jit(solution)/shard_map/while/body/eval_jaxpr/ppermute | solution.py:48
  1415.5 95.7 %collective-permute-start.4 = (f32[768,1024]{1,0:T(8,128)}, f32[768,1024]{1,0:T(8,128)}, u32[]{:S(2)}, u32[]{:S(2)}) collective-permute-start(f32[768,1024]{1,0:T(8,128)} %get-tuple-element.354), channel_id=1, source_target_pairs={{0,1},{1,2},{2,3},{3,4},{4,5},{5,6},{6,7},{7,8},{8,9},{9,10},{10,1... | collective-permute-start | bytes 9437192 | tf_op jit(solution)/shard_map/while/body/eval_jaxpr/ppermute | solution.py:48
  1415.5 87.2 %collective-permute-start = (bf16[768,1024]{1,0:T(8,128)(2,1)}, bf16[768,1024]{1,0:T(8,128)(2,1)S(1)}, u32[]{:S(2)}, u32[]{:S(2)}) collective-permute-start(bf16[768,1024]{1,0:T(8,128)(2,1)} %get-tuple-element.350), channel_id=1, source_target_pairs={{0,1},{1,2},{2,3},{3,4},{4,5},{5,6},{6,7},{7,8},{8,9},{9,10},{10,1... | collective-permute-start | bytes 4718600 | tf_op jit(solution)/shard_map/while/body/eval_jaxpr/ppermute | solution.py:48
  1521.8 95.7 %collective-permute-start.4 = (f32[768,1024]{1,0:T(8,128)}, f32[768,1024]{1,0:T(8,128)}, u32[]{:S(2)}, u32[]{:S(2)}) collective-permute-start(f32[768,1024]{1,0:T(8,128)} %get-tuple-element.354), channel_id=1, source_target_pairs={{0,1},{1,2},{2,3},{3,4},{4,5},{5,6},{6,7},{7,8},{8,9},{9,10},{10,1... | collective-permute-start | bytes 9437192 | tf_op jit(solution)/shard_map/while/body/eval_jaxpr/ppermute | solution.py:48
  1521.8 87.2 %collective-permute-start = (bf16[768,1024]{1,0:T(8,128)(2,1)}, bf16[768,1024]{1,0:T(8,128)(2,1)S(1)}, u32[]{:S(2)}, u32[]{:S(2)}) collective-permute-start(bf16[768,1024]{1,0:T(8,128)(2,1)} %get-tuple-element.350), channel_id=1, source_target_pairs={{0,1},{1,2},{2,3},{3,4},{4,5},{5,6},{6,7},{7,8},{8,9},{9,10},{10,1... | collective-permute-start | bytes 4718600 | tf_op jit(solution)/shard_map/while/body/eval_jaxpr/ppermute | solution.py:48
  1628.1 95.7 %collective-permute-start.4 = (f32[768,1024]{1,0:T(8,128)}, f32[768,1024]{1,0:T(8,128)}, u32[]{:S(2)}, u32[]{:S(2)}) collective-permute-start(f32[768,1024]{1,0:T(8,128)} %get-tuple-element.354), channel_id=1, source_target_pairs={{0,1},{1,2},{2,3},{3,4},{4,5},{5,6},{6,7},{7,8},{8,9},{9,10},{10,1... | collective-permute-start | bytes 9437192 | tf_op jit(solution)/shard_map/while/body/eval_jaxpr/ppermute | solution.py:48
  1628.1 87.2 %collective-permute-start = (bf16[768,1024]{1,0:T(8,128)(2,1)}, bf16[768,1024]{1,0:T(8,128)(2,1)S(1)}, u32[]{:S(2)}, u32[]{:S(2)}) collective-permute-start(bf16[768,1024]{1,0:T(8,128)(2,1)} %get-tuple-element.350), channel_id=1, source_target_pairs={{0,1},{1,2},{2,3},{3,4},{4,5},{5,6},{6,7},{7,8},{8,9},{9,10},{10,1... | collective-permute-start | bytes 4718600 | tf_op jit(solution)/shard_map/while/body/eval_jaxpr/ppermute | solution.py:48
  1734.4 95.7 %collective-permute-start.4 = (f32[768,1024]{1,0:T(8,128)}, f32[768,1024]{1,0:T(8,128)}, u32[]{:S(2)}, u32[]{:S(2)}) collective-permute-start(f32[768,1024]{1,0:T(8,128)} %get-tuple-element.354), channel_id=1, source_target_pairs={{0,1},{1,2},{2,3},{3,4},{4,5},{5,6},{6,7},{7,8},{8,9},{9,10},{10,1... | collective-permute-start | bytes 9437192 | tf_op jit(solution)/shard_map/while/body/eval_jaxpr/ppermute | solution.py:48
  1734.4 87.2 %collective-permute-start = (bf16[768,1024]{1,0:T(8,128)(2,1)}, bf16[768,1024]{1,0:T(8,128)(2,1)S(1)}, u32[]{:S(2)}, u32[]{:S(2)}) collective-permute-start(bf16[768,1024]{1,0:T(8,128)(2,1)} %get-tuple-element.350), channel_id=1, source_target_pairs={{0,1},{1,2},{2,3},{3,4},{4,5},{5,6},{6,7},{7,8},{8,9},{9,10},{10,1... | collective-permute-start | bytes 4718600 | tf_op jit(solution)/shard_map/while/body/eval_jaxpr/ppermute | solution.py:48
  1840.7 95.7 %collective-permute-start.4 = (f32[768,1024]{1,0:T(8,128)}, f32[768,1024]{1,0:T(8,128)}, u32[]{:S(2)}, u32[]{:S(2)}) collective-permute-start(f32[768,1024]{1,0:T(8,128)} %get-tuple-element.354), channel_id=1, source_target_pairs={{0,1},{1,2},{2,3},{3,4},{4,5},{5,6},{6,7},{7,8},{8,9},{9,10},{10,1... | collective-permute-start | bytes 9437192 | tf_op jit(solution)/shard_map/while/body/eval_jaxpr/ppermute | solution.py:48
  1840.7 87.2 %collective-permute-start = (bf16[768,1024]{1,0:T(8,128)(2,1)}, bf16[768,1024]{1,0:T(8,128)(2,1)S(1)}, u32[]{:S(2)}, u32[]{:S(2)}) collective-permute-start(bf16[768,1024]{1,0:T(8,128)(2,1)} %get-tuple-element.350), channel_id=1, source_target_pairs={{0,1},{1,2},{2,3},{3,4},{4,5},{5,6},{6,7},{7,8},{8,9},{9,10},{10,1... | collective-permute-start | bytes 4718600 | tf_op jit(solution)/shard_map/while/body/eval_jaxpr/ppermute | solution.py:48
  1946.9 95.7 %collective-permute-start.4 = (f32[768,1024]{1,0:T(8,128)}, f32[768,1024]{1,0:T(8,128)}, u32[]{:S(2)}, u32[]{:S(2)}) collective-permute-start(f32[768,1024]{1,0:T(8,128)} %get-tuple-element.354), channel_id=1, source_target_pairs={{0,1},{1,2},{2,3},{3,4},{4,5},{5,6},{6,7},{7,8},{8,9},{9,10},{10,1... | collective-permute-start | bytes 9437192 | tf_op jit(solution)/shard_map/while/body/eval_jaxpr/ppermute | solution.py:48
  1947.0 87.2 %collective-permute-start = (bf16[768,1024]{1,0:T(8,128)(2,1)}, bf16[768,1024]{1,0:T(8,128)(2,1)S(1)}, u32[]{:S(2)}, u32[]{:S(2)}) collective-permute-start(bf16[768,1024]{1,0:T(8,128)(2,1)} %get-tuple-element.350), channel_id=1, source_target_pairs={{0,1},{1,2},{2,3},{3,4},{4,5},{5,6},{6,7},{7,8},{8,9},{9,10},{10,1... | collective-permute-start | bytes 4718600 | tf_op jit(solution)/shard_map/while/body/eval_jaxpr/ppermute | solution.py:48
  2053.2 95.7 %collective-permute-start.4 = (f32[768,1024]{1,0:T(8,128)}, f32[768,1024]{1,0:T(8,128)}, u32[]{:S(2)}, u32[]{:S(2)}) collective-permute-start(f32[768,1024]{1,0:T(8,128)} %get-tuple-element.354), channel_id=1, source_target_pairs={{0,1},{1,2},{2,3},{3,4},{4,5},{5,6},{6,7},{7,8},{8,9},{9,10},{10,1... | collective-permute-start | bytes 9437192 | tf_op jit(solution)/shard_map/while/body/eval_jaxpr/ppermute | solution.py:48
  2053.3 87.2 %collective-permute-start = (bf16[768,1024]{1,0:T(8,128)(2,1)}, bf16[768,1024]{1,0:T(8,128)(2,1)S(1)}, u32[]{:S(2)}, u32[]{:S(2)}) collective-permute-start(bf16[768,1024]{1,0:T(8,128)(2,1)} %get-tuple-element.350), channel_id=1, source_target_pairs={{0,1},{1,2},{2,3},{3,4},{4,5},{5,6},{6,7},{7,8},{8,9},{9,10},{10,1... | collective-permute-start | bytes 4718600 | tf_op jit(solution)/shard_map/while/body/eval_jaxpr/ppermute | solution.py:48
  2159.5 95.7 %collective-permute-start.4 = (f32[768,1024]{1,0:T(8,128)}, f32[768,1024]{1,0:T(8,128)}, u32[]{:S(2)}, u32[]{:S(2)}) collective-permute-start(f32[768,1024]{1,0:T(8,128)} %get-tuple-element.354), channel_id=1, source_target_pairs={{0,1},{1,2},{2,3},{3,4},{4,5},{5,6},{6,7},{7,8},{8,9},{9,10},{10,1... | collective-permute-start | bytes 9437192 | tf_op jit(solution)/shard_map/while/body/eval_jaxpr/ppermute | solution.py:48
  2159.6 87.2 %collective-permute-start = (bf16[768,1024]{1,0:T(8,128)(2,1)}, bf16[768,1024]{1,0:T(8,128)(2,1)S(1)}, u32[]{:S(2)}, u32[]{:S(2)}) collective-permute-start(bf16[768,1024]{1,0:T(8,128)(2,1)} %get-tuple-element.350), channel_id=1, source_target_pairs={{0,1},{1,2},{2,3},{3,4},{4,5},{5,6},{6,7},{7,8},{8,9},{9,10},{10,1... | collective-permute-start | bytes 4718600 | tf_op jit(solution)/shard_map/while/body/eval_jaxpr/ppermute | solution.py:48
  2265.8 95.7 %collective-permute-start.4 = (f32[768,1024]{1,0:T(8,128)}, f32[768,1024]{1,0:T(8,128)}, u32[]{:S(2)}, u32[]{:S(2)}) collective-permute-start(f32[768,1024]{1,0:T(8,128)} %get-tuple-element.354), channel_id=1, source_target_pairs={{0,1},{1,2},{2,3},{3,4},{4,5},{5,6},{6,7},{7,8},{8,9},{9,10},{10,1... | collective-permute-start | bytes 9437192 | tf_op jit(solution)/shard_map/while/body/eval_jaxpr/ppermute | solution.py:48
  2265.8 87.2 %collective-permute-start = (bf16[768,1024]{1,0:T(8,128)(2,1)}, bf16[768,1024]{1,0:T(8,128)(2,1)S(1)}, u32[]{:S(2)}, u32[]{:S(2)}) collective-permute-start(bf16[768,1024]{1,0:T(8,128)(2,1)} %get-tuple-element.350), channel_id=1, source_target_pairs={{0,1},{1,2},{2,3},{3,4},{4,5},{5,6},{6,7},{7,8},{8,9},{9,10},{10,1... | collective-permute-start | bytes 4718600 | tf_op jit(solution)/shard_map/while/body/eval_jaxpr/ppermute | solution.py:48
  2372.1 95.7 %collective-permute-start.4 = (f32[768,1024]{1,0:T(8,128)}, f32[768,1024]{1,0:T(8,128)}, u32[]{:S(2)}, u32[]{:S(2)}) collective-permute-start(f32[768,1024]{1,0:T(8,128)} %get-tuple-element.354), channel_id=1, source_target_pairs={{0,1},{1,2},{2,3},{3,4},{4,5},{5,6},{6,7},{7,8},{8,9},{9,10},{10,1... | collective-permute-start | bytes 9437192 | tf_op jit(solution)/shard_map/while/body/eval_jaxpr/ppermute | solution.py:48
  2372.1 87.2 %collective-permute-start = (bf16[768,1024]{1,0:T(8,128)(2,1)}, bf16[768,1024]{1,0:T(8,128)(2,1)S(1)}, u32[]{:S(2)}, u32[]{:S(2)}) collective-permute-start(bf16[768,1024]{1,0:T(8,128)(2,1)} %get-tuple-element.350), channel_id=1, source_target_pairs={{0,1},{1,2},{2,3},{3,4},{4,5},{5,6},{6,7},{7,8},{8,9},{9,10},{10,1... | collective-permute-start | bytes 4718600 | tf_op jit(solution)/shard_map/while/body/eval_jaxpr/ppermute | solution.py:48
  2478.4 95.7 %collective-permute-start.4 = (f32[768,1024]{1,0:T(8,128)}, f32[768,1024]{1,0:T(8,128)}, u32[]{:S(2)}, u32[]{:S(2)}) collective-permute-start(f32[768,1024]{1,0:T(8,128)} %get-tuple-element.354), channel_id=1, source_target_pairs={{0,1},{1,2},{2,3},{3,4},{4,5},{5,6},{6,7},{7,8},{8,9},{9,10},{10,1... | collective-permute-start | bytes 9437192 | tf_op jit(solution)/shard_map/while/body/eval_jaxpr/ppermute | solution.py:48
  2478.4 87.2 %collective-permute-start = (bf16[768,1024]{1,0:T(8,128)(2,1)}, bf16[768,1024]{1,0:T(8,128)(2,1)S(1)}, u32[]{:S(2)}, u32[]{:S(2)}) collective-permute-start(bf16[768,1024]{1,0:T(8,128)(2,1)} %get-tuple-element.350), channel_id=1, source_target_pairs={{0,1},{1,2},{2,3},{3,4},{4,5},{5,6},{6,7},{7,8},{8,9},{9,10},{10,1... | collective-permute-start | bytes 4718600 | tf_op jit(solution)/shard_map/while/body/eval_jaxpr/ppermute | solution.py:48
  2584.7 95.7 %collective-permute-start.4 = (f32[768,1024]{1,0:T(8,128)}, f32[768,1024]{1,0:T(8,128)}, u32[]{:S(2)}, u32[]{:S(2)}) collective-permute-start(f32[768,1024]{1,0:T(8,128)} %get-tuple-element.354), channel_id=1, source_target_pairs={{0,1},{1,2},{2,3},{3,4},{4,5},{5,6},{6,7},{7,8},{8,9},{9,10},{10,1... | collective-permute-start | bytes 9437192 | tf_op jit(solution)/shard_map/while/body/eval_jaxpr/ppermute | solution.py:48
  2584.7 87.2 %collective-permute-start = (bf16[768,1024]{1,0:T(8,128)(2,1)}, bf16[768,1024]{1,0:T(8,128)(2,1)S(1)}, u32[]{:S(2)}, u32[]{:S(2)}) collective-permute-start(bf16[768,1024]{1,0:T(8,128)(2,1)} %get-tuple-element.350), channel_id=1, source_target_pairs={{0,1},{1,2},{2,3},{3,4},{4,5},{5,6},{6,7},{7,8},{8,9},{9,10},{10,1... | collective-permute-start | bytes 4718600 | tf_op jit(solution)/shard_map/while/body/eval_jaxpr/ppermute | solution.py:48
  2691.0 95.7 %collective-permute-start.4 = (f32[768,1024]{1,0:T(8,128)}, f32[768,1024]{1,0:T(8,128)}, u32[]{:S(2)}, u32[]{:S(2)}) collective-permute-start(f32[768,1024]{1,0:T(8,128)} %get-tuple-element.354), channel_id=1, source_target_pairs={{0,1},{1,2},{2,3},{3,4},{4,5},{5,6},{6,7},{7,8},{8,9},{9,10},{10,1... | collective-permute-start | bytes 9437192 | tf_op jit(solution)/shard_map/while/body/eval_jaxpr/ppermute | solution.py:48
  2691.0 87.2 %collective-permute-start = (bf16[768,1024]{1,0:T(8,128)(2,1)}, bf16[768,1024]{1,0:T(8,128)(2,1)S(1)}, u32[]{:S(2)}, u32[]{:S(2)}) collective-permute-start(bf16[768,1024]{1,0:T(8,128)(2,1)} %get-tuple-element.350), channel_id=1, source_target_pairs={{0,1},{1,2},{2,3},{3,4},{4,5},{5,6},{6,7},{7,8},{8,9},{9,10},{10,1... | collective-permute-start | bytes 4718600 | tf_op jit(solution)/shard_map/while/body/eval_jaxpr/ppermute | solution.py:48
  2797.3 95.7 %collective-permute-start.4 = (f32[768,1024]{1,0:T(8,128)}, f32[768,1024]{1,0:T(8,128)}, u32[]{:S(2)}, u32[]{:S(2)}) collective-permute-start(f32[768,1024]{1,0:T(8,128)} %get-tuple-element.354), channel_id=1, source_target_pairs={{0,1},{1,2},{2,3},{3,4},{4,5},{5,6},{6,7},{7,8},{8,9},{9,10},{10,1... | collective-permute-start | bytes 9437192 | tf_op jit(solution)/shard_map/while/body/eval_jaxpr/ppermute | solution.py:48
  2797.3 87.2 %collective-permute-start = (bf16[768,1024]{1,0:T(8,128)(2,1)}, bf16[768,1024]{1,0:T(8,128)(2,1)S(1)}, u32[]{:S(2)}, u32[]{:S(2)}) collective-permute-start(bf16[768,1024]{1,0:T(8,128)(2,1)} %get-tuple-element.350), channel_id=1, source_target_pairs={{0,1},{1,2},{2,3},{3,4},{4,5},{5,6},{6,7},{7,8},{8,9},{9,10},{10,1... | collective-permute-start | bytes 4718600 | tf_op jit(solution)/shard_map/while/body/eval_jaxpr/ppermute | solution.py:48
  2903.6 95.7 %collective-permute-start.4 = (f32[768,1024]{1,0:T(8,128)}, f32[768,1024]{1,0:T(8,128)}, u32[]{:S(2)}, u32[]{:S(2)}) collective-permute-start(f32[768,1024]{1,0:T(8,128)} %get-tuple-element.354), channel_id=1, source_target_pairs={{0,1},{1,2},{2,3},{3,4},{4,5},{5,6},{6,7},{7,8},{8,9},{9,10},{10,1... | collective-permute-start | bytes 9437192 | tf_op jit(solution)/shard_map/while/body/eval_jaxpr/ppermute | solution.py:48
  2903.6 87.2 %collective-permute-start = (bf16[768,1024]{1,0:T(8,128)(2,1)}, bf16[768,1024]{1,0:T(8,128)(2,1)S(1)}, u32[]{:S(2)}, u32[]{:S(2)}) collective-permute-start(bf16[768,1024]{1,0:T(8,128)(2,1)} %get-tuple-element.350), channel_id=1, source_target_pairs={{0,1},{1,2},{2,3},{3,4},{4,5},{5,6},{6,7},{7,8},{8,9},{9,10},{10,1... | collective-permute-start | bytes 4718600 | tf_op jit(solution)/shard_map/while/body/eval_jaxpr/ppermute | solution.py:48
  3009.8 95.7 %collective-permute-start.4 = (f32[768,1024]{1,0:T(8,128)}, f32[768,1024]{1,0:T(8,128)}, u32[]{:S(2)}, u32[]{:S(2)}) collective-permute-start(f32[768,1024]{1,0:T(8,128)} %get-tuple-element.354), channel_id=1, source_target_pairs={{0,1},{1,2},{2,3},{3,4},{4,5},{5,6},{6,7},{7,8},{8,9},{9,10},{10,1... | collective-permute-start | bytes 9437192 | tf_op jit(solution)/shard_map/while/body/eval_jaxpr/ppermute | solution.py:48
  3009.9 87.2 %collective-permute-start = (bf16[768,1024]{1,0:T(8,128)(2,1)}, bf16[768,1024]{1,0:T(8,128)(2,1)S(1)}, u32[]{:S(2)}, u32[]{:S(2)}) collective-permute-start(bf16[768,1024]{1,0:T(8,128)(2,1)} %get-tuple-element.350), channel_id=1, source_target_pairs={{0,1},{1,2},{2,3},{3,4},{4,5},{5,6},{6,7},{7,8},{8,9},{9,10},{10,1... | collective-permute-start | bytes 4718600 | tf_op jit(solution)/shard_map/while/body/eval_jaxpr/ppermute | solution.py:48
  3116.1 95.7 %collective-permute-start.4 = (f32[768,1024]{1,0:T(8,128)}, f32[768,1024]{1,0:T(8,128)}, u32[]{:S(2)}, u32[]{:S(2)}) collective-permute-start(f32[768,1024]{1,0:T(8,128)} %get-tuple-element.354), channel_id=1, source_target_pairs={{0,1},{1,2},{2,3},{3,4},{4,5},{5,6},{6,7},{7,8},{8,9},{9,10},{10,1... | collective-permute-start | bytes 9437192 | tf_op jit(solution)/shard_map/while/body/eval_jaxpr/ppermute | solution.py:48
  (109 other events, 5331.9 us)
where the time goes:
time: 3330 us; the launch traced here: 3290 us
  local copies, waits for them, and re-layouts  1730 us (52%)
  waiting for transfers between devices  1110 us (33%)
  other arithmetic  211 us (6%)
  matrix products  167 us (5%)
  starting transfers between devices  70.4 us (2%)
    ppermute x150, waiting for transfers between devices, pass_on(): visitor, accum = lax.ppermute((visitor, accum), 'ep', next_perm)  1110 us
    scatter x32, local copies, waits for them, and re-layouts, local_share(): jnp.zeros((num_local * shard_cap,), jnp.float32).at[flat_slot]  735 us
    scatter x32, local copies, waits for them, and re-layouts, local_share(): jnp.full((num_local * shard_cap,), tok_dev, jnp.int32).at[flat_slot]  735 us
    scatter-add x32, other arithmetic, local_share(): jnp.zeros((tok_dev, token_blk.shape[1]), jnp.float32).at[slot_token]  205 us
    while x150, local copies, waits for them, and re-layouts  156 us
    dot_general x32, matrix products, local_share(): jnp.einsum('ecf,efd->ecd', hidden, w_down, preferred_element_type=jnp.flo...  87 us
    dot_general x31, matrix products, local_share(): jnp.einsum('ecd,edf->ecf', dispatched, w_up, preferred_element_type=jnp.f...  77.2 us
    gather x32, local copies, waits for them, and re-layouts, local_share(): jnp.take(token_blk, slot_token, axis=0, mode='fill', fill_value=0)  71.3 us
  transfers between devices with their start and end apart: 155, of which 39 were waited for; matrix products, arithmetic and copies ran while one was open for 54% of the time, Pallas kernels for 0%

commit v1 on v0

v1 whole, which is shorter than its diff:
```python
import functools
import math
import jax
import jax.numpy as jnp
from jax import lax
from jax.experimental import pallas as pl
from jax.experimental.pallas import tpu as pltpu
from jax.sharding import PartitionSpec as P

CORES = 2
MESH_ID = pl.DeviceIdType.MESH
PIECES = 4
GU_TILES = 2
DN_TILES = 2

W_SENDS = ((0, 'w', 0), (0, 'w', 1), (1, 'w', 0), (0, 'w', 2), (1, 'w', 1), (0, 'w', 3),
           (0, 'd', 0), (0, 'd', 2), (1, 'd', 0), (0, 'd', 1), (0, 'd', 3), (1, 'd', 1))
W_ISSUE = ((2, 3), (4,), (5,), (6,), (7,), (), (8, 9), (10,), (), (11,), (), ())


def moe_kernel(side, tok_ref, ids_ref, gates_ref, slots_ref, wg_ref, wu_ref, wd_ref, out_ref,
               x, gt, gcol, wgu, wdn, h, part, recv0,
               load_sem, d2d_send, d2d_recv, wr_send, wr_recv, wl_send, wl_recv,
               tr_send, tr_recv, tl_send, tl_recv, rs_send, rs_recv, credit):
    me = lax.axis_index('ep')
    core = lax.rem(me, CORES)
    xx = lax.rem(me // CORES, side)
    yy = me // (CORES * side)
    wi = yy * (1 - core) + xx * core
    ti = xx * (1 - core) + yy * core

    def dev(w_pos, t_pos):
        y_pos = w_pos * (1 - core) + t_pos * core
        x_pos = t_pos * (1 - core) + w_pos * core
        return {'ep': (y_pos * side + x_pos) * CORES + core}

    def ring(pos, off):
        return lax.rem(pos + off + 2 * side, side)

    w_next, w_prev = dev(ring(wi, 1), ti), dev(ring(wi, -1), ti)
    t_next, t_prev = dev(wi, ring(ti, 1)), dev(wi, ring(ti, -1))
    partner = {'ep': me + 1 - 2 * core}

    rows, width = x.shape[1], x.shape[2]
    half = rows // 2
    ff = h.shape[3]
    fp = ff // PIECES
    dp = width // PIECES
    num_q = h.shape[1]

    loads = {}
    for i in range(PIECES):
        for k, src in enumerate((wg_ref, wu_ref)):
            loads['w', i, k] = pltpu.make_async_copy(
                src.at[0, :, pl.ds(i * fp, fp)], wgu.at[wi, i, core, :, pl.ds(k * fp, fp)], load_sem.at[2 * i + k])
        loads['d', i] = pltpu.make_async_copy(
            wd_ref.at[0, :, pl.ds(i * dp, dp)], wdn.at[wi, i, core], load_sem.at[2 * PIECES + i])
    for c in range(2):
        loads['x', c] = pltpu.make_async_copy(
            tok_ref.at[pl.ds(c * half, half)], x.at[ti, pl.ds(c * half, half)], load_sem.at[3 * PIECES + c])
    for c in range(2):
        loads['x', c].start()
    for i in (0, 2, 1, 3):
        loads['w', i, 0].start()
        loads['w', i, 1].start()
    for i in (0, 2, 1, 3):
        loads['d', i].start()

    barrier = pltpu.get_barrier_semaphore()
    for peer in (w_next, w_prev, t_next, t_prev, partner):
        pl.semaphore_signal(barrier, inc=1, device_id=peer, device_id_type=MESH_ID)
    pl.semaphore_wait(barrier, 5)

    def remote(src, dst, s_sem, r_sem, peer):
        return pltpu.make_async_remote_copy(src_ref=src, dst_ref=dst, send_sem=s_sem, recv_sem=r_sem,
                                            device_id=peer, device_id_type=MESH_ID)

    def w_piece(kind, slot, piece):
        return (wgu if kind == 'w' else wdn).at[slot, piece]

    def w_copy(right, n):
        fwd, kind, piece = W_SENDS[n]
        if right:
            ref = w_piece(kind, ring(wi, -fwd), piece)
            return remote(ref, ref, wr_send.at[n], wr_recv.at[n], w_next)
        ref = w_piece(kind, ring(wi, fwd), piece ^ 2)
        return remote(ref, ref, wl_send.at[n], wl_recv.at[n], w_prev)

    def w_wait(n):
        fwd, kind, piece = W_SENDS[n]
        ref = w_piece(kind, ring(wi, -1 - fwd), piece)
        remote(ref, ref, wr_send.at[n], wr_recv.at[n], w_next).wait_recv()
        ref = w_piece(kind, ring(wi, 1 + fwd), piece ^ 2)
        remote(ref, ref, wl_send.at[n], wl_recv.at[n], w_prev).wait_recv()

    def w_issue(n):
        for pos in W_ISSUE[n]:
            w_copy(True, pos).start()
            w_copy(False, pos).start()

    T_RIGHT = ((0, 'x', 0), (0, 'x', 1), (0, 'g', 0), (1, 'x', 0), (1, 'g', 0))
    T_LEFT = ((0, 'x', 1), (0, 'x', 0), (0, 'g', 0), (1, 'x', 1))

    def t_piece(kind, slot, c):
        return x.at[slot, pl.ds(c * half, half)] if kind == 'x' else gt.at[slot]

    def t_copy(right, n):
        fwd, kind, c = (T_RIGHT if right else T_LEFT)[n]
        if right:
            ref = t_piece(kind, ring(ti, -fwd), c)
            return remote(ref, ref, tr_send.at[n], tr_recv.at[n], t_next)
        ref = t_piece(kind, ring(ti, fwd), c)
        return remote(ref, ref, tl_send.at[n], tl_recv.at[n], t_prev)

    def t_wait(right, n):
        fwd, kind, c = (T_RIGHT if right else T_LEFT)[n]
        if right:
            ref = t_piece(kind, ring(ti, -1 - fwd), c)
            remote(ref, ref, tr_send.at[n], tr_recv.at[n], t_next).wait_recv()
        else:
            ref = t_piece(kind, ring(ti, 1 + fwd), c)
            remote(ref, ref, tl_send.at[n], tl_recv.at[n], t_prev).wait_recv()

    loads['x', 0].wait()
    t_copy(True, 0).start()
    loads['x', 1].wait()
    t_copy(False, 0).start()
    t_copy(True, 1).start()
    t_copy(False, 1).start()

    def d2d(kind, i, incoming):
        n = i + (0 if kind == 'w' else PIECES)
        ref = wgu if kind == 'w' else wdn
        mine = ref.at[wi, i, core]
        dst = ref.at[wi, i, 1 - core] if incoming else ref.at[ti, i, core]
        return remote(mine, dst, d2d_send.at[n], d2d_recv.at[n], partner)

    for i in (0, 2, 1, 3):
        loads['w', i, 0].wait()
        loads['w', i, 1].wait()
        d2d('w', i, False).start()
    for i in (0, 2, 1, 3):
        loads['d', i].wait()
        d2d('d', i, False).start()
    for n in range(2):
        d2d('w', n, True).wait_recv()
        w_copy(True, n).start()
        d2d('w', n ^ 2, True).wait_recv()
        w_copy(False, n).start()

    lane = lax.broadcasted_iota(jnp.int32, (gt.shape[1], 1), 0)
    l_t, l_w, l_c = lane // (CORES * side), lax.rem(lane // CORES, side), lax.rem(lane, CORES)
    e_y = l_w * (1 - core) + l_t * core
    e_x = l_t * (1 - core) + l_w * core
    expert = (e_y * side + e_x) * CORES + l_c
    dense = jnp.full(gt.shape[1:], jnp.nan, jnp.float32)
    for j in range(ids_ref.shape[0]):
        hit = (ids_ref[j:j + 1, :] == expert) & (slots_ref[j:j + 1, :] >= 0)
        dense = jnp.where(hit, gates_ref[j:j + 1, :], dense)
    gt[ti] = dense

    for i in (0, 2, 1, 3):
        d2d('d', i, True).wait_recv()

    gu_rows = rows // GU_TILES
    dn_rows = rows // DN_TILES

    def gate_up(shard, hs, slot, piece, cc, rt):
        r = pl.ds(pl.multiple_of(rt * gu_rows, gu_rows), gu_rows)
        both = jnp.dot(x[shard, r, :], wgu[slot, piece, cc], preferred_element_type=jnp.float32)
        a, u = both[:, :fp], both[:, fp:]
        hid = (a * jax.nn.sigmoid(a)) * u
        h[hs, slot * CORES + cc, r, pl.ds(pl.multiple_of(piece * fp, fp), fp)] = hid.astype(jnp.bfloat16)

    def near(s):
        return ring(ti, 2 * s - 1)

    def near_own():
        def body(t, carry):
            s, t2 = t // (PIECES * CORES * GU_TILES), lax.rem(t, PIECES * CORES * GU_TILES)
            piece, t3 = t2 // (CORES * GU_TILES), lax.rem(t2, CORES * GU_TILES)
            gate_up(near(s), s, wi, piece, t3 // GU_TILES, lax.rem(t3, GU_TILES))
            return carry
        lax.fori_loop(0, 2 * PIECES * CORES * GU_TILES, body, 0)

    def arrived(n, d):
        fwd, _, piece = W_SENDS[n]
        return ring(wi, (2 * d - 1) * (1 + fwd)), piece + d * ((piece ^ 2) - piece)

    def near_arrived(n):
        def body(t, carry):
            d, t2 = t // (2 * CORES * GU_TILES), lax.rem(t, 2 * CORES * GU_TILES)
            s, t3 = t2 // (CORES * GU_TILES), lax.rem(t2, CORES * GU_TILES)
            slot, piece = arrived(n, d)
            gate_up(near(s), s, slot, piece, t3 // GU_TILES, lax.rem(t3, GU_TILES))
            return carry
        lax.fori_loop(0, 4 * CORES * GU_TILES, body, 0)

    def whole(shard, hs, first, last):
        per = PIECES * CORES * GU_TILES
        def body(t, carry):
            s, t2 = t // per, lax.rem(t, per)
            piece, t3 = t2 // (CORES * GU_TILES), lax.rem(t2, CORES * GU_TILES)
            gate_up(shard, hs, ring(wi, s), piece, t3 // GU_TILES, lax.rem(t3, GU_TILES))
            return carry
        lax.fori_loop(first * per, last * per, body, 0)

    def far_arrived(n):
        def body(t, carry):
            d, t3 = t // (CORES * GU_TILES), lax.rem(t, CORES * GU_TILES)
            slot, piece = arrived(n, d)
            gate_up(ring(ti, 2), 2, slot, piece, t3 // GU_TILES, lax.rem(t3, GU_TILES))
            return carry
        lax.fori_loop(0, 2 * CORES * GU_TILES, body, 0)

    def gates_to_columns():
        base = pl.ds(pl.multiple_of(ti * num_q, num_q), num_q)
        for s in range(side):
            gcol[s] = jnp.transpose(gt[s, base, :])

    def down(shard, hs, chunk, r, start):
        acc = start
        for q in range(num_q):
            o = jnp.dot(h[hs, q, r, :], wdn[q // CORES, chunk, q % CORES], preferred_element_type=jnp.float32)
            g = jnp.broadcast_to(gcol[shard, r, q:q + 1], o.shape)
            term = jnp.where(g == g, g * o, 0.0)
            acc = term if acc is None else acc + term
        return acc

    def near_down(base, flip):
        def body(t, carry):
            s, rt = t // DN_TILES, lax.rem(t, DN_TILES)
            r = pl.ds(pl.multiple_of(rt * dn_rows, dn_rows), dn_rows)
            shard = s if not flip else 1 - s
            chunk = base + 2 * s
            part[shard, chunk, r, :] = down(near(shard), shard, chunk, r, None)
            return carry
        lax.fori_loop(0, 2 * DN_TILES, body, 0)

    def rs_copy(step, j):
        right = j < 2
        sent = part.at[0, j] if right else part.at[1, j]
        kept = part.at[1, j] if right else part.at[0, j]
        src, dst = ((sent, recv0.at[j]), (recv0.at[j], sent), (sent, kept))[step]
        return remote(src, dst, rs_send.at[step, j], rs_recv.at[step, j], t_next if right else t_prev)

    def give_credit(step, j):
        pl.semaphore_signal(credit.at[step, j], inc=1, device_id=t_prev if j < 2 else t_next, device_id_type=MESH_ID)

    t_wait(True, 0)
    t_wait(False, 0)
    t_copy(True, 2).start()
    t_copy(False, 2).start()
    t_copy(True, 3).start()
    t_copy(False, 3).start()
    w_wait(0)
    w_issue(0)
    t_wait(True, 1)
    t_wait(False, 1)
    near_own()
    w_wait(1)
    w_issue(1)
    near_arrived(0)
    near_arrived(1)
    t_wait(True, 2)
    t_wait(False, 2)
    t_copy(True, 4).start()
    w_wait(2)
    w_issue(2)
    near_arrived(2)
    w_wait(3)
    w_issue(3)
    near_arrived(3)
    t_wait(True, 3)
    t_wait(False, 3)
    t_wait(True, 4)
    gates_to_columns()
    whole(ring(ti, 2), 2, 0, 1)
    w_wait(4)
    w_issue(4)
    near_arrived(4)
    far_arrived(0)
    far_arrived(1)
    w_wait(5)
    w_issue(5)
    near_arrived(5)
    far_arrived(2)
    far_arrived(3)
    w_wait(6)
    w_issue(6)
    far_arrived(4)
    w_wait(7)
    w_issue(7)
    far_arrived(5)
    w_wait(8)
    w_issue(8)
    near_down(0, False)
    rs_copy(0, 0).start()
    rs_copy(0, 2).start()
    w_wait(9)
    w_issue(9)
    near_down(0, True)
    w_wait(10)
    w_wait(11)
    near_down(1, False)
    rs_copy(0, 1).start()
    rs_copy(0, 3).start()
    near_down(1, True)

    far = ring(ti, 2)

    def turn_far(j):
        for k in (j, j + 2):
            rs_copy(0, k).wait_send()
            give_credit(0, k)
        for k in (j, j + 2):
            rs_copy(0, k).wait_recv()

        def body(t, carry):
            chunk, rt = j + 2 * (t // DN_TILES), lax.rem(t, DN_TILES)
            r = pl.ds(pl.multiple_of(rt * dn_rows, dn_rows), dn_rows)
            recv0[chunk, r, :] = down(far, 2, chunk, r, recv0[chunk, r, :])
            return carry
        lax.fori_loop(0, 2 * DN_TILES, body, 0)
        for k in (j, j + 2):
            pl.semaphore_wait(credit.at[0, k], 1)
            rs_copy(1, k).start()

    def turn_near(j):
        for k in (j, j + 2):
            rs_copy(1, k).wait_recv()
        part[0, j] = part[0, j] + part[1, j]
        part[1, j + 2] = part[1, j + 2] + part[0, j + 2]
        for k in (j, j + 2):
            give_credit(1, k)
        for k in (j, j + 2):
            pl.semaphore_wait(credit.at[1, k], 1)
            rs_copy(2, k).start()

    turn_far(0)
    turn_far(1)
    whole(ti, 0, 0, side // 2)
    turn_near(0)
    whole(ti, 0, side // 2, side)
    turn_near(1)
    for j in (0, 2, 1, 3):
        rs_copy(1, j).wait_send()

    def own_body(t, carry):
        chunk, rt = t // DN_TILES, lax.rem(t, DN_TILES)
        r = pl.ds(pl.multiple_of(rt * dn_rows, dn_rows), dn_rows)
        recv0[chunk, r, :] = down(ti, 0, chunk, r, None)
        return carry
    lax.fori_loop(0, PIECES * DN_TILES, own_body, 0)

    for j in (0, 2, 1, 3):
        rs_copy(2, j).wait_recv()
        kept = part[1, j] if j < 2 else part[0, j]
        out_ref[:, j * dp:(j + 1) * dp] = (recv0[j] + kept).astype(out_ref.dtype)

    for j in range(PIECES):
        rs_copy(2, j).wait_send()
    for n in range(len(W_SENDS)):
        w_copy(True, n).wait_send()
        w_copy(False, n).wait_send()
    for n in range(len(T_RIGHT)):
        t_copy(True, n).wait_send()
    for n in range(len(T_LEFT)):
        t_copy(False, n).wait_send()
    for i in range(PIECES):
        d2d('w', i, False).wait_send()
        d2d('d', i, False).wait_send()


def solution(mesh):
    group = mesh.shape['ep']
    side = math.isqrt(group // CORES)
    row_spec = P(('dp', 'ep'), None)
    expert_spec = P('ep', None, None)

    def per_device(tokens, expert_ids, gate_wts, slot_ids, w_gate, w_up, w_down):
        rows, width = tokens.shape
        ff = w_gate.shape[2]
        num_q = CORES * side
        fp, dp = ff // PIECES, width // PIECES
        dma = pltpu.SemaphoreType.DMA
        hbm = pl.BlockSpec(memory_space=pl.ANY)
        vmem = pl.BlockSpec(memory_space=pltpu.VMEM)
        n_w = len(W_SENDS)
        return pl.pallas_call(
            functools.partial(moe_kernel, side),
            out_shape=jax.ShapeDtypeStruct((rows, width), jnp.bfloat16),
            in_specs=[hbm, vmem, vmem, vmem, hbm, hbm, hbm],
            out_specs=vmem,
            scratch_shapes=[
                pltpu.VMEM((side, rows, width), jnp.bfloat16),
                pltpu.VMEM((side, group, rows), jnp.float32),
                pltpu.VMEM((side, rows, num_q), jnp.float32),
                pltpu.VMEM((side, PIECES, CORES, width, 2 * fp), jnp.bfloat16),
                pltpu.VMEM((side, PIECES, CORES, ff, dp), jnp.bfloat16),
                pltpu.VMEM((3, num_q, rows, ff), jnp.bfloat16),
                pltpu.VMEM((2, PIECES, rows, dp), jnp.float32),
                pltpu.VMEM((PIECES, rows, dp), jnp.float32),
                dma((3 * PIECES + 2,)), dma((2 * PIECES,)), dma((2 * PIECES,)),
                dma((n_w,)), dma((n_w,)), dma((n_w,)), dma((n_w,)),
                dma((5,)), dma((5,)), dma((4,)), dma((4,)),
                dma((3, PIECES)), dma((3, PIECES)),
                pltpu.SemaphoreType.REGULAR((2, PIECES)),
            ],
            compiler_params=pltpu.CompilerParams(collective_id=0, has_side_effects=True, vmem_limit_bytes=67043328),
        )(tokens, expert_ids.T, gate_wts.T, slot_ids.T, w_gate, w_up, w_down)

    return jax.shard_map(per_device, mesh=mesh, in_specs=(row_spec, row_spec, row_spec, row_spec, expert_spec, expert_spec, expert_spec), out_specs=row_spec, check_vma=False)
```

time: 3330 us -> 218 us (0.07); the launches traced: 3290 us -> 218 us
  local copies, waits for them, and re-layouts: 1730 us -> 2.67 us
  waiting for transfers between devices: 1110 us -> 0 us
  Pallas kernels: 0 us -> 215 us
  other arithmetic: 211 us -> 0 us
  matrix products: 167 us -> 0 us
  starting transfers between devices: 70.4 us -> 0 us
    scatter x64 -> x0, local copies, waits for them, and re-layouts: 1470 us -> none  [the longest x32 735 us: local_share(): jnp.zeros((num_local * shard_cap,), jnp.float32).at[flat_slot]]
    ppermute x155 -> x0, waiting for transfers between devices: 1110 us -> none  [the longest x150 1110 us: pass_on(): visitor, accum = lax.ppermute((visitor, accum), 'ep', next_perm)]
    pallas_call x0 -> x1, Pallas kernels: none -> 215 us  [per_device(): pl.pallas_call(functools.partial(moe_kernel, side), out_shape=jax.ShapeDt...]
    scatter-add x32 -> x0, other arithmetic: 205 us -> none  [local_share(): jnp.zeros((tok_dev, token_blk.shape[1]), jnp.float32).at[slot_token]]
    dot_general x64 -> x0, matrix products: 167 us -> none  [the longest x32 87 us: local_share(): jnp.einsum('ecf,efd->ecd', hidden, w_down, preferred_element_type=jnp.flo...]
    while x150 -> x0, local copies, waits for them, and re-layouts: 156 us -> none
    gather x32 -> x0, local copies, waits for them, and re-layouts: 71.3 us -> none  [local_share(): jnp.take(token_blk, slot_token, axis=0, mode='fill', fill_value=0)]
    ppermute x155 -> x0, starting transfers between devices: 70.4 us -> none  [the longest x150 65.9 us: pass_on(): visitor, accum = lax.ppermute((visitor, accum), 'ep', next_perm)]
  transfers between devices with their start and end apart: 155 -> 0, of which waited for: 39 -> 0; matrix products, arithmetic and copies ran while one was open for 54% -> 0% of each run, Pallas kernels for 0% -> 0%
where the time goes in v1:
time: 218 us
  Pallas kernels  215 us (99%)
  local copies, waits for them, and re-layouts  2.67 us (1%)
    pallas_call x1, Pallas kernels, per_device(): pl.pallas_call(functools.partial(moe_kernel, side), out_shape=jax.ShapeDt...  215 us

profile of v1, /device:TPU:97, one launch (start us, length us, event | category | flops | bytes accessed | tf_op | source)
XLA Modules:
  0.0 217.6 jit_solution(5192108124934171284)
XLA Ops:
  0.0 214.9 %shard_map.73 = bf16[768,1024]{1,0:T(8,128)(2,1)} custom-call(bf16[768,1024]{1,0:T(8,128)(2,1)} %tok_ref.1, s32[8,768]{1,0:T(8,128)} %bitcast.3, f32[8,768]{1,0:T(8,128)} %bitcast.4, s32[8,768]{1,0:T(8,128)} %bitcast.5, bf16[1,1024,512]{2,1,0:T(8,128)(2,1)} %wg_ref.1, bf16[1,1024,512]{2,1,0:T(8,128)(2,1)} %wu_ref.1, bf16[1,512,1024]{2,1,0:T(8,128)(2,1)} %wd_ref.1), custom_call_target="tpu_custom_call" | custom-call | tf_op jit(solution)/shard_map/pallas_call | solution.py:390
  214.9 2.7 %copy.9 = bf16[768,1024]{1,0:T(8,128)(2,1)} copy(bf16[768,1024]{1,0:T(8,128)(2,1)} %shard_map.73) | data formatting | bytes 3145728

commit v2 on v1

v2 whole, which is shorter than its diff:
```python
import functools
import math
import jax
import jax.numpy as jnp
from jax import lax
from jax.experimental import pallas as pl
from jax.experimental.pallas import tpu as pltpu
from jax.sharding import PartitionSpec as P

CORES = 2
MESH_ID = pl.DeviceIdType.MESH
PIECES = 4
HALVES = 2

W_SENDS = ((0, 'w', 0), (0, 'w', 1), (1, 'w', 0), (0, 'w', 2), (1, 'w', 1), (0, 'w', 3),
           (0, 'd', 0), (0, 'd', 2), (1, 'd', 0), (0, 'd', 1), (0, 'd', 3), (1, 'd', 1))
W_ISSUE = ((2, 3), (4,), (5,), (6,), (7,), (), (8, 9), (10,), (), (11,), (), ())


def moe_kernel(side, tok_ref, ids_ref, gates_ref, slots_ref, wg_ref, wu_ref, wd_ref, out_ref,
               x, gown, gt, gfwd, gcol, wgu, wdn, h, part, recv0,
               load_sem, d2d_send, d2d_recv, wr_send, wr_recv, wl_send, wl_recv,
               tr_send, tr_recv, tl_send, tl_recv, rs_send, rs_recv, credit):
    me = lax.axis_index('ep')
    core = lax.rem(me, CORES)
    xx = lax.rem(me // CORES, side)
    yy = me // (CORES * side)
    wi = yy * (1 - core) + xx * core
    ti = xx * (1 - core) + yy * core

    def dev(w_pos, t_pos):
        y_pos = w_pos * (1 - core) + t_pos * core
        x_pos = t_pos * (1 - core) + w_pos * core
        return {'ep': (y_pos * side + x_pos) * CORES + core}

    def ring(pos, off):
        return lax.rem(pos + off + 2 * side, side)

    w_next, w_prev = dev(ring(wi, 1), ti), dev(ring(wi, -1), ti)
    t_next, t_prev = dev(wi, ring(ti, 1)), dev(wi, ring(ti, -1))
    partner = {'ep': me + 1 - 2 * core}

    rows, width = x.shape[1], x.shape[2]
    half = rows // 2
    ff = h.shape[2]
    fp = ff // PIECES
    dp = width // PIECES
    num_q = CORES * side

    loads = {}
    for i in range(PIECES):
        for k, src in enumerate((wg_ref, wu_ref)):
            loads['w', i, k] = pltpu.make_async_copy(
                src.at[0, :, pl.ds(i * fp, fp)], wgu.at[wi, i, core, :, pl.ds(k * fp, fp)], load_sem.at[2 * i + k])
        loads['d', i] = pltpu.make_async_copy(
            wd_ref.at[0, :, pl.ds(i * dp, dp)], wdn.at[wi, i, core], load_sem.at[2 * PIECES + i])
    for c in range(2):
        loads['x', c] = pltpu.make_async_copy(
            tok_ref.at[pl.ds(c * half, half)], x.at[ti, pl.ds(c * half, half)], load_sem.at[3 * PIECES + c])
    for c in range(2):
        loads['x', c].start()
    for i in (0, 2, 1, 3):
        loads['w', i, 0].start()
        loads['w', i, 1].start()
    for i in (0, 2, 1, 3):
        loads['d', i].start()

    barrier = pltpu.get_barrier_semaphore()
    for peer in (w_next, w_prev, t_next, t_prev, partner):
        pl.semaphore_signal(barrier, inc=1, device_id=peer, device_id_type=MESH_ID)
    pl.semaphore_wait(barrier, 5)

    def remote(src, dst, s_sem, r_sem, peer):
        return pltpu.make_async_remote_copy(src_ref=src, dst_ref=dst, send_sem=s_sem, recv_sem=r_sem,
                                            device_id=peer, device_id_type=MESH_ID)

    def w_piece(kind, slot, piece):
        return (wgu if kind == 'w' else wdn).at[slot, piece]

    def w_copy(right, n):
        fwd, kind, piece = W_SENDS[n]
        if right:
            ref = w_piece(kind, ring(wi, -fwd), piece)
            return remote(ref, ref, wr_send.at[n], wr_recv.at[n], w_next)
        ref = w_piece(kind, ring(wi, fwd), piece ^ 2)
        return remote(ref, ref, wl_send.at[n], wl_recv.at[n], w_prev)

    def w_wait(n):
        fwd, kind, piece = W_SENDS[n]
        ref = w_piece(kind, ring(wi, -1 - fwd), piece)
        remote(ref, ref, wr_send.at[n], wr_recv.at[n], w_next).wait_recv()
        ref = w_piece(kind, ring(wi, 1 + fwd), piece ^ 2)
        remote(ref, ref, wl_send.at[n], wl_recv.at[n], w_prev).wait_recv()

    def w_issue(n):
        for pos in W_ISSUE[n]:
            w_copy(True, pos).start()
            w_copy(False, pos).start()

    def gate_rows(off):
        return gown.at[pl.ds(off * num_q, num_q)]

    def t_refs(right, n, me_t):
        if n in (0, 1):
            ref = x.at[me_t, pl.ds((n if right else 1 - n) * half, half)]
            return ref, ref
        if not right:
            ref = x.at[ring(me_t, 1), pl.ds(half, half)]
            return (gate_rows(side - 1), gt.at[me_t]) if n == 2 else (ref, ref)
        ref = x.at[ring(me_t, -1), pl.ds(0, half)]
        return ((gate_rows(1), gt.at[me_t]), (gate_rows(2), gfwd), (ref, ref), (gfwd, gt.at[ring(me_t, -1)]))[n - 2]

    def t_copy(right, n):
        src, dst = t_refs(right, n, ti)
        if right:
            return remote(src, dst, tr_send.at[n], tr_recv.at[n], t_next)
        return remote(src, dst, tl_send.at[n], tl_recv.at[n], t_prev)

    def t_wait(right, n):
        _, dst = t_refs(right, n, ring(ti, -1 if right else 1))
        if right:
            remote(dst, dst, tr_send.at[n], tr_recv.at[n], t_next).wait_recv()
        else:
            remote(dst, dst, tl_send.at[n], tl_recv.at[n], t_prev).wait_recv()

    loads['x', 0].wait()
    t_copy(True, 0).start()
    loads['x', 1].wait()
    t_copy(False, 0).start()
    t_copy(True, 1).start()
    t_copy(False, 1).start()

    def d2d(kind, i, incoming):
        n = i + (0 if kind == 'w' else PIECES)
        ref = wgu if kind == 'w' else wdn
        mine = ref.at[wi, i, core]
        dst = ref.at[wi, i, 1 - core] if incoming else ref.at[ti, i, core]
        return remote(mine, dst, d2d_send.at[n], d2d_recv.at[n], partner)

    for i in (0, 2, 1, 3):
        loads['w', i, 0].wait()
        loads['w', i, 1].wait()
        d2d('w', i, False).start()
    for i in (0, 2, 1, 3):
        loads['d', i].wait()
        d2d('d', i, False).start()
    for n in range(2):
        d2d('w', n, True).wait_recv()
        w_copy(True, n).start()
        d2d('w', n ^ 2, True).wait_recv()
        w_copy(False, n).start()

    line = lax.broadcasted_iota(jnp.int32, (gown.shape[0], 1), 0)
    l_t, l_w, l_c = lax.rem(line // num_q + ti, side), lax.rem(line // CORES + wi, side), lax.rem(line, CORES)
    e_y = l_w * (1 - core) + l_t * core
    e_x = l_t * (1 - core) + l_w * core
    expert = (e_y * side + e_x) * CORES + l_c
    dense = jnp.full(gown.shape, jnp.nan, jnp.float32)
    for j in range(ids_ref.shape[0]):
        hit = (ids_ref[j:j + 1, :] == expert) & (slots_ref[j:j + 1, :] >= 0)
        dense = jnp.where(hit, gates_ref[j:j + 1, :], dense)
    gown[...] = dense
    gt[ti] = dense[:num_q]

    for i in (0, 2, 1, 3):
        d2d('d', i, True).wait_recv()

    hr = rows // HALVES

    def half_rows(rt):
        return pl.ds(rt * hr, hr)

    def gate_up(shard, base, k, piece):
        slot = ring(wi, k)
        for cc in range(CORES):
            both = jnp.dot(x[shard], wgu[slot, piece, cc], preferred_element_type=jnp.float32)
            a, u = both[:, :fp], both[:, fp:]
            hid = (a / (1.0 + jnp.exp(-a))) * u
            h[base + k * CORES + cc, :, pl.ds(pl.multiple_of(piece * fp, fp), fp)] = hid.astype(jnp.bfloat16)

    FAR = 2 * num_q
    OWN = (3 * num_q, 0)

    def near(s):
        return ring(ti, 2 * s - 1)

    def arrived(n, d):
        fwd, _, piece = W_SENDS[n]
        return side - 1 - fwd + d * (2 + 2 * fwd - side), piece + d * ((piece ^ 2) - piece)

    def near_own():
        def body(t, carry):
            s = lax.rem(t, 2)
            gate_up(near(s), s * num_q, 0, t // 2)
            return carry
        lax.fori_loop(0, 2 * PIECES, body, 0)

    def near_arrived(n):
        def body(t, carry):
            k, piece = arrived(n, t // 2)
            s = lax.rem(t, 2)
            gate_up(near(s), s * num_q, k, piece)
            return carry
        lax.fori_loop(0, 4, body, 0)

    def far_arrived(n):
        def body(t, carry):
            k, piece = arrived(n, t)
            gate_up(far, FAR, k, piece)
            return carry
        lax.fori_loop(0, 2, body, 0)

    def all_pieces(shard, base, first, last):
        def body(t, carry):
            gate_up(shard, base, t // PIECES, lax.rem(t, PIECES))
            return carry
        lax.fori_loop(first * PIECES, last * PIECES, body, 0)

    def gates_to_columns():
        for s, other in ((0, far), (1, ti)):
            gcol[s] = jnp.transpose(jnp.concatenate([gt[near(s)], gt[other]], axis=0))

    far = ring(ti, 2)

    def down(gates, bases, chunk, r, start):
        g_at, g_off = gates
        acc = start
        for q in range(num_q):
            k, cc = q // CORES, q % CORES
            base = bases[k // (side // 2)]
            o = jnp.dot(h[base + q, r, :], wdn[ring(wi, k), chunk, cc], preferred_element_type=jnp.float32)
            g = jnp.broadcast_to(gcol[g_at, r, g_off + q:g_off + q + 1], o.shape)
            term = jnp.where(g == g, g * o, 0.0)
            acc = term if acc is None else acc + term
        return acc

    def near_down(base, rt, flip):
        r = half_rows(rt)

        def body(s, carry):
            shard = s if not flip else 1 - s
            chunk = base + 2 * s
            part[shard, chunk, r, :] = down((shard, 0), (shard * num_q,) * 2, chunk, r, None)
            return carry
        lax.fori_loop(0, 2, body, 0)

    def rs_copy(step, j, rt):
        right = j < 2
        r = half_rows(rt)
        sent = part.at[0 if right else 1, j, r]
        kept = part.at[1 if right else 0, j, r]
        held = recv0.at[j, r]
        src, dst = ((sent, held), (held, sent), (sent, kept))[step]
        return remote(src, dst, rs_send.at[step, j, rt], rs_recv.at[step, j, rt], t_next if right else t_prev)

    def give_credit(step, j, rt):
        pl.semaphore_signal(credit.at[step, j, rt], inc=1, device_id=t_prev if j < 2 else t_next, device_id_type=MESH_ID)

    def first_send(j):
        for rt in range(HALVES):
            near_down(j, rt, False)
            rs_copy(0, j, rt).start()
            rs_copy(0, j + 2, rt).start()

    def keep(j):
        for rt in range(HALVES):
            near_down(j, rt, True)

    def turn_far(j, rt):
        r = half_rows(rt)
        for k in (j, j + 2):
            rs_copy(0, k, rt).wait_send()
            give_credit(0, k, rt)
        for k in (j, j + 2):
            rs_copy(0, k, rt).wait_recv()

        def body(t, carry):
            chunk = j + 2 * t
            recv0[chunk, r, :] = down((0, num_q), (FAR,) * 2, chunk, r, recv0[chunk, r, :])
            return carry
        lax.fori_loop(0, 2, body, 0)
        for k in (j, j + 2):
            pl.semaphore_wait(credit.at[0, k, rt], 1)
            rs_copy(1, k, rt).start()

    def turn_near(j, rt):
        r = half_rows(rt)
        for k in (j, j + 2):
            rs_copy(1, k, rt).wait_recv()
            s = k // 2
            part[s, k, r, :] = part[s, k, r, :] + part[1 - s, k, r, :]
            give_credit(1, k, rt)
        for k in (j, j + 2):
            pl.semaphore_wait(credit.at[1, k, rt], 1)
            rs_copy(2, k, rt).start()

    def own_down(j):
        for k in (j, j + 2):
            for rt in range(HALVES):
                rs_copy(1, k, rt).wait_send()

        def body(t, carry):
            chunk = j + 2 * (t // HALVES)
            r = pl.ds(pl.multiple_of(lax.rem(t, HALVES) * hr, hr), hr)
            recv0[chunk, r, :] = down((1, num_q), OWN, chunk, r, None)
            return carry
        lax.fori_loop(0, 2 * HALVES, body, 0)

    def finish(j, rt):
        r = half_rows(rt)
        for k in (j, j + 2):
            rs_copy(2, k, rt).wait_recv()
            out_ref[r, k * dp:(k + 1) * dp] = (recv0[k, r, :] + part[1 - k // 2, k, r, :]).astype(out_ref.dtype)

    half_k = side // 2
    all_pieces(ti, OWN[0], 0, 1)
    t_wait(True, 0)
    t_wait(False, 0)
    t_copy(True, 2).start()
    t_copy(False, 2).start()
    t_copy(True, 3).start()
    t_copy(True, 4).start()
    t_copy(False, 3).start()
    w_wait(0)
    w_issue(0)
    t_wait(True, 1)
    t_wait(False, 1)
    near_own()
    w_wait(1)
    w_issue(1)
    near_arrived(0)
    near_arrived(1)
    t_wait(True, 2)
    t_wait(False, 2)
    t_wait(True, 3)
    t_copy(True, 5).start()
    w_wait(2)
    w_issue(2)
    near_arrived(2)
    w_wait(3)
    w_issue(3)
    near_arrived(3)
    t_wait(True, 4)
    t_wait(False, 3)
    t_wait(True, 5)
    gates_to_columns()
    all_pieces(far, FAR, 0, 1)
    w_wait(4)
    w_issue(4)
    near_arrived(4)
    far_arrived(0)
    far_arrived(1)
    w_wait(5)
    w_issue(5)
    near_arrived(5)
    far_arrived(2)
    far_arrived(3)
    w_wait(6)
    w_issue(6)
    far_arrived(4)
    w_wait(7)
    w_issue(7)
    far_arrived(5)
    w_wait(8)
    w_issue(8)
    first_send(0)
    w_wait(9)
    w_issue(9)
    keep(0)
    all_pieces(ti, OWN[0], 1, half_k)
    turn_far(0, 0)
    turn_far(0, 1)
    w_wait(10)
    w_wait(11)
    first_send(1)
    keep(1)
    turn_near(0, 0)
    turn_near(0, 1)
    turn_far(1, 0)
    turn_far(1, 1)
    all_pieces(ti, OWN[1], half_k, side)
    own_down(0)
    turn_near(1, 0)
    turn_near(1, 1)
    own_down(1)
    for j in range(2):
        for rt in range(HALVES):
            finish(j, rt)

    for j in range(PIECES):
        for rt in range(HALVES):
            rs_copy(2, j, rt).wait_send()
    for n in range(len(W_SENDS)):
        w_copy(True, n).wait_send()
        w_copy(False, n).wait_send()
    for n in range(6):
        t_copy(True, n).wait_send()
    for n in range(4):
        t_copy(False, n).wait_send()
    for i in range(PIECES):
        d2d('w', i, False).wait_send()
        d2d('d', i, False).wait_send()


def solution(mesh):
    group = mesh.shape['ep']
    side = math.isqrt(group // CORES)
    row_spec = P(('dp', 'ep'), None)
    expert_spec = P('ep', None, None)

    def per_device(tokens, expert_ids, gate_wts, slot_ids, w_gate, w_up, w_down):
        rows, width = tokens.shape
        ff = w_gate.shape[2]
        num_q = CORES * side
        fp, dp = ff // PIECES, width // PIECES
        dma = pltpu.SemaphoreType.DMA
        hbm = pl.BlockSpec(memory_space=pl.ANY)
        vmem = pl.BlockSpec(memory_space=pltpu.VMEM)
        n_w = len(W_SENDS)
        return pl.pallas_call(
            functools.partial(moe_kernel, side),
            out_shape=jax.ShapeDtypeStruct((rows, width), jnp.bfloat16),
            in_specs=[hbm, vmem, vmem, vmem, hbm, hbm, hbm],
            out_specs=vmem,
            scratch_shapes=[
                pltpu.VMEM((side, rows, width), jnp.bfloat16),
                pltpu.VMEM((group, rows), jnp.float32),
                pltpu.VMEM((side, num_q, rows), jnp.float32),
                pltpu.VMEM((num_q, rows), jnp.float32),
                pltpu.VMEM((2, rows, 2 * num_q), jnp.float32),
                pltpu.VMEM((side, PIECES, CORES, width, 2 * fp), jnp.bfloat16),
                pltpu.VMEM((side, PIECES, CORES, ff, dp), jnp.bfloat16),
                pltpu.VMEM((3 * num_q + num_q // 2, rows, ff), jnp.bfloat16),
                pltpu.VMEM((2, PIECES, rows, dp), jnp.float32),
                pltpu.VMEM((PIECES, rows, dp), jnp.float32),
                dma((3 * PIECES + 2,)), dma((2 * PIECES,)), dma((2 * PIECES,)),
                dma((n_w,)), dma((n_w,)), dma((n_w,)), dma((n_w,)),
                dma((6,)), dma((6,)), dma((4,)), dma((4,)),
                dma((3, PIECES, HALVES)), dma((3, PIECES, HALVES)),
                pltpu.SemaphoreType.REGULAR((2, PIECES, HALVES)),
            ],
            compiler_params=pltpu.CompilerParams(collective_id=0, has_side_effects=True, vmem_limit_bytes=67043328),
        )(tokens, expert_ids.T, gate_wts.T, slot_ids.T, w_gate, w_up, w_down)

    return jax.shard_map(per_device, mesh=mesh, in_specs=(row_spec, row_spec, row_spec, row_spec, expert_spec, expert_spec, expert_spec), out_specs=row_spec, check_vma=False)
```

time: 218 us -> 197 us (0.904)
  Pallas kernels: 215 us -> 194 us
    pallas_call x1, Pallas kernels: 215 us -> 194 us  [per_device(): pl.pallas_call(functools.partial(moe_kernel, side), out_shape=jax.ShapeDt...]
where the time goes in v2:
time: 197 us
  Pallas kernels  194 us (98%)
  local copies, waits for them, and re-layouts  2.67 us (1%)
    pallas_call x1, Pallas kernels, per_device(): pl.pallas_call(functools.partial(moe_kernel, side), out_shape=jax.ShapeDt...  194 us

profile of v2, /device:TPU:97, one launch (start us, length us, event | category | flops | bytes accessed | tf_op | source)
XLA Modules:
  0.0 197.0 jit_solution(6787486349164572918)
XLA Ops:
  0.0 194.3 %shard_map.73 = bf16[768,1024]{1,0:T(8,128)(2,1)} custom-call(bf16[768,1024]{1,0:T(8,128)(2,1)} %tok_ref.1, s32[8,768]{1,0:T(8,128)} %bitcast.3, f32[8,768]{1,0:T(8,128)} %bitcast.4, s32[8,768]{1,0:T(8,128)} %bitcast.5, bf16[1,1024,512]{2,1,0:T(8,128)(2,1)} %wg_ref.1, bf16[1,1024,512]{2,1,0:T(8,128)(2,1)} %wu_ref.1, bf16[1,512,1024]{2,1,0:T(8,128)(2,1)} %wd_ref.1), custom_call_target="tpu_custom_call" | custom-call | tf_op jit(solution)/shard_map/pallas_call | solution.py:420
  194.3 2.7 %copy.9 = bf16[768,1024]{1,0:T(8,128)(2,1)} copy(bf16[768,1024]{1,0:T(8,128)(2,1)} %shard_map.73) | data formatting | bytes 3145728

commit v3 on v2

--- a/solution.py
+++ b/solution.py
@@ -379,8 +379,8 @@
     turn_far(1, 0)
     turn_far(1, 1)
     all_pieces(ti, OWN[1], half_k, side)
+    turn_near(1, 0)
     own_down(0)
-    turn_near(1, 0)
     turn_near(1, 1)
     own_down(1)
     for j in range(2):
@@ -402,6 +402,12 @@
         d2d('d', i, False).wait_send()
 
 
+def place_kernel(src_ref, dst_ref, sem):
+    copy = pltpu.make_async_copy(src_ref, dst_ref, sem.at[0])
+    copy.start()
+    copy.wait()
+
+
 def solution(mesh):
     group = mesh.shape['ep']
     side = math.isqrt(group // CORES)
@@ -417,9 +423,9 @@
         hbm = pl.BlockSpec(memory_space=pl.ANY)
         vmem = pl.BlockSpec(memory_space=pltpu.VMEM)
         n_w = len(W_SENDS)
-        return pl.pallas_call(
+        result = pl.pallas_call(
             functools.partial(moe_kernel, side),
-            out_shape=jax.ShapeDtypeStruct((rows, width), jnp.bfloat16),
+            out_shape=pltpu.VMEM((rows, width), jnp.bfloat16),
             in_specs=[hbm, vmem, vmem, vmem, hbm, hbm, hbm],
             out_specs=vmem,
             scratch_shapes=[
@@ -439,7 +445,15 @@
                 dma((3, PIECES, HALVES)), dma((3, PIECES, HALVES)),
                 pltpu.SemaphoreType.REGULAR((2, PIECES, HALVES)),
             ],
-            compiler_params=pltpu.CompilerParams(collective_id=0, has_side_effects=True, vmem_limit_bytes=67043328),
+            compiler_params=pltpu.CompilerParams(collective_id=0, has_side_effects=True, vmem_limit_bytes=67043328 - rows * width * 2),
         )(tokens, expert_ids.T, gate_wts.T, slot_ids.T, w_gate, w_up, w_down)
+        return pl.pallas_call(
+            place_kernel,
+            out_shape=jax.ShapeDtypeStruct((rows, width), jnp.bfloat16),
+            in_specs=[vmem],
+            out_specs=hbm,
+            scratch_shapes=[dma((1,))],
+            compiler_params=pltpu.CompilerParams(vmem_limit_bytes=1 << 20),
+        )(result)
 
     return jax.shard_map(per_device, mesh=mesh, in_specs=(row_spec, row_spec, row_spec, row_spec, expert_spec, expert_spec, expert_spec), out_specs=row_spec, check_vma=False)

time: 197 us -> 194 us (0.985)
  local copies, waits for them, and re-layouts: 2.67 us -> 0 us
    unnamed x1 -> x0, local copies, waits for them, and re-layouts: 2.67 us -> none
    pallas_call x1 -> x2, Pallas kernels: 194 us -> 193 us  [the longest x1 192 us: per_device(): pl.pallas_call(functools.partial(moe_kernel, side), out_shape=pltpu.VMEM(...]
where the time goes in v3:
time: 194 us
  Pallas kernels  193 us (99%)
    pallas_call x1, Pallas kernels, per_device(): pl.pallas_call(functools.partial(moe_kernel, side), out_shape=pltpu.VMEM(...  192 us

profile of v3, /device:TPU:97, one launch (start us, length us, event | category | flops | bytes accessed | tf_op | source)
XLA Modules:
  0.0 193.6 jit_solution(11732044347301880500)
XLA Ops:
  0.0 192.2 %shard_map.73.src_ref = bf16[768,1024]{1,0:T(8,128)(2,1)S(1)} custom-call(bf16[768,1024]{1,0:T(8,128)(2,1)} %tok_ref.1, s32[8,768]{1,0:T(8,128)} %bitcast.3, f32[8,768]{1,0:T(8,128)} %bitcast.4, s32[8,768]{1,0:T(8,128)} %bitcast.5, bf16[1,1024,512]{2,1,0:T(8,128)(2,1)} %wg_ref.1, bf16[1,1024,512]{2,1,0:T(8,128)(2,1)} %wu_ref.1, bf16[1,512,1024]{2,1,0:T(8,128)(2,1)} %wd_ref.1), custom_call_target="tpu_custom_call" | custom-call | tf_op jit(solution)/shard_map/pallas_call | solution.py:426
  192.2 1.2 shard_map.74

commit v4 on v3

--- a/solution.py
+++ b/solution.py
@@ -222,25 +222,30 @@
 
     far = ring(ti, 2)
 
-    def down(gates, bases, chunk, r, start):
+    ALL_K = tuple(range(side))
+    LAST_K = (side // 2,)
+    EARLY_K = tuple(k for k in ALL_K if k not in LAST_K)
+
+    def down(gates, bases, chunk, r, start, ks=ALL_K):
         g_at, g_off = gates
         acc = start
-        for q in range(num_q):
-            k, cc = q // CORES, q % CORES
-            base = bases[k // (side // 2)]
-            o = jnp.dot(h[base + q, r, :], wdn[ring(wi, k), chunk, cc], preferred_element_type=jnp.float32)
-            g = jnp.broadcast_to(gcol[g_at, r, g_off + q:g_off + q + 1], o.shape)
-            term = jnp.where(g == g, g * o, 0.0)
-            acc = term if acc is None else acc + term
+        for k in ks:
+            for q in range(k * CORES, (k + 1) * CORES):
+                h_row = bases[k // (side // 2)] + q
+                o = jnp.dot(h[h_row, r, :], wdn[ring(wi, k), chunk, q % CORES], preferred_element_type=jnp.float32)
+                g = jnp.broadcast_to(gcol[g_at, r, g_off + q:g_off + q + 1], o.shape)
+                term = jnp.where(g == g, g * o, 0.0)
+                acc = term if acc is None else acc + term
         return acc
 
-    def near_down(base, rt, flip):
+    def near_down(base, rt, flip, ks=ALL_K, more=False):
         r = half_rows(rt)
 
         def body(s, carry):
             shard = s if not flip else 1 - s
             chunk = base + 2 * s
-            part[shard, chunk, r, :] = down((shard, 0), (shard * num_q,) * 2, chunk, r, None)
+            start = part[shard, chunk, r, :] if more else None
+            part[shard, chunk, r, :] = down((shard, 0), (shard * num_q,) * 2, chunk, r, start, ks)
             return carry
         lax.fori_loop(0, 2, body, 0)
 
@@ -256,9 +261,13 @@
     def give_credit(step, j, rt):
         pl.semaphore_signal(credit.at[step, j, rt], inc=1, device_id=t_prev if j < 2 else t_next, device_id_type=MESH_ID)
 
+    def first_part(j):
+        for rt in range(HALVES):
+            near_down(j, rt, False, EARLY_K)
+
     def first_send(j):
         for rt in range(HALVES):
-            near_down(j, rt, False)
+            near_down(j, rt, False, LAST_K, True)
             rs_copy(0, j, rt).start()
             rs_copy(0, j + 2, rt).start()
 
@@ -360,10 +369,11 @@
     far_arrived(4)
     w_wait(7)
     w_issue(7)
-    far_arrived(5)
+    first_part(0)
     w_wait(8)
     w_issue(8)
     first_send(0)
+    far_arrived(5)
     w_wait(9)
     w_issue(9)
     keep(0)
@@ -371,6 +381,7 @@
     turn_far(0, 0)
     turn_far(0, 1)
     w_wait(10)
+    first_part(1)
     w_wait(11)
     first_send(1)
     keep(1)
@@ -383,13 +394,12 @@
     own_down(0)
     turn_near(1, 1)
     own_down(1)
-    for j in range(2):
-        for rt in range(HALVES):
-            finish(j, rt)
-
+    finish(0, 0)
+    finish(0, 1)
     for j in range(PIECES):
         for rt in range(HALVES):
-            rs_copy(2, j, rt).wait_send()
+            if j % 2 == 0 or rt == 0:
+                rs_copy(2, j, rt).wait_send()
     for n in range(len(W_SENDS)):
         w_copy(True, n).wait_send()
         w_copy(False, n).wait_send()
@@ -400,6 +410,10 @@
     for i in range(PIECES):
         d2d('w', i, False).wait_send()
         d2d('d', i, False).wait_send()
+    finish(1, 0)
+    finish(1, 1)
+    for j in range(1, PIECES, 2):
+        rs_copy(2, j, 1).wait_send()
 
 
 def place_kernel(src_ref, dst_ref, sem):

time: 194 us -> 193 us (level)
  no operation moved by 1% of the time
where the time goes in v4:
time: 193 us
  Pallas kernels  193 us (100%)
    pallas_call x1, Pallas kernels, per_device(): pl.pallas_call(functools.partial(moe_kernel, side), out_shape=pltpu.VMEM(...  192 us

profile of v4, /device:TPU:97, one launch (start us, length us, event | category | flops | bytes accessed | tf_op | source)
XLA Modules:
  0.0 192.9 jit_solution(16641668443777409624)
XLA Ops:
  0.0 191.6 %shard_map.73.src_ref = bf16[768,1024]{1,0:T(8,128)(2,1)S(1)} custom-call(bf16[768,1024]{1,0:T(8,128)(2,1)} %tok_ref.1, s32[8,768]{1,0:T(8,128)} %bitcast.3, f32[8,768]{1,0:T(8,128)} %bitcast.4, s32[8,768]{1,0:T(8,128)} %bitcast.5, bf16[1,1024,512]{2,1,0:T(8,128)(2,1)} %wg_ref.1, bf16[1,1024,512]{2,1,0:T(8,128)(2,1)} %wu_ref.1, bf16[1,512,1024]{2,1,0:T(8,128)(2,1)} %wd_ref.1), custom_call_target="tpu_custom_call" | custom-call | tf_op jit(solution)/shard_map/pallas_call | solution.py:440
  191.6 1.2 shard_map.74
